TPU v7x, 32 devices: a whole 2x2x4 slice. The times are simulated.
32 devices in a mesh: facet: 4 (over z), chan: 8 (over y, x, core).
Axes of the slice: x: 2, y: 2, z: 4, core: 2. Of those that a mesh axis runs over, the one named last changes fastest.
Arguments:
- visibilities: bfloat16 [2, 8, 256, 32, 128], P(None, None, None, ('facet', 'chan')), may hold values from -12 to 12
- kernels: bfloat16 [32, 256, 512], replicated, may hold values from -0.25 to 0.25
- delays: float32 [8, 256, 128], P('facet'), may hold values from -4 to 4
- tile_of: int32 [8, 256], P('facet'), may hold values from 0 to 127
- plane_of: int32 [8, 256], P('facet'), may hold values from 0 to 31
- counts: int32 [8], P('facet'), may hold values from 64 to 256
- neighbours: int32 [8, 4], replicated, may hold values from 0 to 7, as said below
Outputs:
- joined_grids: float32 [128, 8, 4, 512], P('chan', 'facet')
Inputs may be any that keep to these rules, and one draw needn't show every extreme that they name: `neighbours`: each row names 4 different facets, none of them its own.
All inputs are finite; a program needn't handle non-finite values.
Results may differ from a plain program's by a relative error of at most 0.0043.
Values may be sent and summed in bfloat16 or wider, within the bound.
A program may use at most 128 MiB of HBM per device.

v0:
```python
import math
import jax
import jax.numpy as jnp
from jax import lax
from jax.sharding import PartitionSpec as P

AVG = 8
TS = 16
NT_DEV = 16
GROUP = 8
EDGE = 4
HIGHEST = lax.Precision.HIGHEST


def average_group(vis_piece, delay_piece, freq_turn, avg_matrix):
    vis_float = vis_piece.astype(jnp.float32)
    phase_angle = delay_piece[:, None, :] * freq_turn[None, :, None]
    cosine = jnp.cos(phase_angle)
    sine_part = jnp.sin(phase_angle)
    rot_real = vis_float[0] * cosine - vis_float[1] * sine_part
    rot_imag = vis_float[0] * sine_part + vis_float[1] * cosine
    avg_real = jnp.einsum("oc,gcv->gov", avg_matrix, rot_real, precision=HIGHEST)
    avg_imag = jnp.einsum("oc,gcv->gov", avg_matrix, rot_imag, precision=HIGHEST)
    return jnp.concatenate([avg_real, avg_imag], axis=-1).astype(jnp.bfloat16)


def project_rows(row_list, plane_list, kernels):
    products = []
    for row_item, plane_item in zip(row_list, plane_list):
        matrix = lax.dynamic_index_in_dim(kernels, plane_item, 0, keepdims=False)
        products.append(jnp.dot(row_item, matrix, preferred_element_type=jnp.float32))
    return jnp.stack(products, axis=0)


def add_tiles(grid_acc, contrib, tile_piece, weight, n_tiles):
    table = (tile_piece[None, :] == jnp.arange(n_tiles, dtype=jnp.int32)[:, None]).astype(
        jnp.float32
    ) * weight[None, :]
    return grid_acc + jnp.einsum("tg,gcx->tcx", table, contrib, precision=HIGHEST)


def grid_facet(
    vis_slot,
    delay_slot,
    tiles_slot,
    planes_slot,
    live_count,
    kernels,
    freq_turn,
    avg_matrix,
    n_tiles,
):
    group_size = GROUP
    out_chan = avg_matrix.shape[0]
    wide_cells = kernels.shape[2]

    def accumulate(step_index, grid_acc):
        begin_row = step_index * group_size
        vis_piece = lax.dynamic_slice_in_dim(vis_slot, begin_row, group_size, 1)
        delay_piece = lax.dynamic_slice_in_dim(delay_slot, begin_row, group_size, 0)
        avg_rows = average_group(vis_piece, delay_piece, freq_turn, avg_matrix)
        plane_piece = lax.dynamic_slice_in_dim(planes_slot, begin_row, group_size, 0)
        contrib = project_rows(
            [avg_rows[g] for g in range(group_size)],
            [plane_piece[g] for g in range(group_size)],
            kernels,
        )
        block_ids = begin_row + jnp.arange(group_size, dtype=jnp.int32)
        live_mask = (block_ids < live_count).astype(jnp.float32)
        tile_piece = lax.dynamic_slice_in_dim(tiles_slot, begin_row, group_size, 0)
        return add_tiles(grid_acc, contrib, tile_piece, live_mask, n_tiles)

    trip_count = (live_count + group_size - 1) // group_size
    start_grid = jnp.zeros((n_tiles, out_chan, wide_cells), jnp.float32)
    return lax.fori_loop(0, trip_count, accumulate, start_grid)


def local(visibilities, kernels, delays, tile_of, plane_of, counts, neighbours):
    n_facet = lax.axis_size("facet")
    n_chan = lax.axis_size("chan")
    facet_index = lax.axis_index("facet")
    chan_index = lax.axis_index("chan")
    halves, facets, blocks, ch_dev, block_vis = visibilities.shape
    fac_dev = facets // n_facet
    blk_dev = blocks // n_chan
    channels = ch_dev * n_facet * n_chan
    out_chan = channels // AVG
    tile_cells = kernels.shape[2] // 2
    n_tiles = NT_DEV * n_chan
    edge_cells = EDGE * TS
    reshaped = visibilities.reshape(halves, n_facet, fac_dev, blk_dev, n_chan, ch_dev, block_vis)
    arranged = jnp.transpose(reshaped, (0, 1, 4, 2, 3, 5, 6))
    my_delays = lax.dynamic_index_in_dim(
        delays.reshape(fac_dev, blk_dev, n_chan, block_vis), chan_index, 2, keepdims=False
    )
    my_tiles = lax.dynamic_index_in_dim(
        tile_of.reshape(fac_dev, blk_dev, n_chan), chan_index, 2, keepdims=False
    )
    my_planes = lax.dynamic_index_in_dim(
        plane_of.reshape(fac_dev, blk_dev, n_chan), chan_index, 2, keepdims=False
    )
    my_live = jnp.clip((counts - chan_index + n_chan - 1) // n_chan, 0, blk_dev)
    position = jnp.arange(channels, dtype=jnp.int32)
    flattened = arranged.reshape(halves, n_facet * n_chan, fac_dev, blk_dev, ch_dev, block_vis)
    received = lax.all_to_all(flattened, ("facet", "chan"), split_axis=1, concat_axis=4, tiled=True)
    local_vis = received.reshape(halves, fac_dev, blk_dev, channels, block_vis)
    freq_turn = 2.0 * math.pi * (1.0 + 0.5 * position.astype(jnp.float32) / channels)
    avg_matrix = (
        position[None, :] // AVG == jnp.arange(out_chan, dtype=jnp.int32)[:, None]
    ).astype(jnp.float32) / AVG
    facet_grids = []
    for facet_slot in range(fac_dev):
        facet_grids.append(
            grid_facet(
                local_vis[:, facet_slot],
                my_delays[facet_slot],
                my_tiles[facet_slot],
                my_planes[facet_slot],
                my_live[facet_slot],
                kernels,
                freq_turn,
                avg_matrix,
                n_tiles,
            )
        )
    stacked = jnp.stack(facet_grids, axis=1)
    summed = lax.psum_scatter(stacked, "chan", scatter_dimension=0, tiled=True)
    strips = jnp.concatenate(
        [summed[..., :edge_cells], summed[..., tile_cells : tile_cells + edge_cells]], axis=-1
    )
    gathered = lax.all_gather(strips.astype(jnp.bfloat16), "facet", axis=1, tiled=True).astype(
        strips.dtype
    )
    my_neighbours = lax.dynamic_slice_in_dim(neighbours, facet_index * fac_dev, fac_dev, 0)
    adjacency = jnp.sum(
        (my_neighbours[:, :, None] == jnp.arange(facets, dtype=jnp.int32)[None, None, :]).astype(
            jnp.float32
        ),
        axis=1,
    )
    blended = 0.25 * jnp.einsum("fg,tgcx->tfcx", adjacency, gathered, precision=HIGHEST)
    joined = summed.at[..., tile_cells - edge_cells : tile_cells].add(blended[..., :edge_cells])
    joined = joined.at[..., 2 * tile_cells - edge_cells :].add(blended[..., edge_cells:])
    return joined


def solution(mesh):
    return jax.shard_map(
        local,
        mesh=mesh,
        in_specs=(
            P(None, None, None, ("facet", "chan"), None),
            P(),
            P("facet", None, None),
            P("facet", None),
            P("facet", None),
            P("facet"),
            P(),
        ),
        out_specs=P("chan", "facet", None, None),
        check_vma=False,
    )
```

profile of v0, /device:TPU:0, one launch (start us, length us, event | category | flops | bytes accessed | tf_op | source)
XLA Modules:
  0.0 319.1 jit_solution(13530689246377154184)
XLA Ops:
  6.5 2.5 copy.46
  9.0 7.3 %all-to-all-start = ((bf16[2,32,2,32,1,128]{5,3,0,2,4,1:T(8,128)(2,1)}), bf16[2,32,2,32,1,128]{5,3,0,2,4,1:T(8,128)(2,1)S(1)}, u32[]{:S(2)}, u32[]{:S(2)}) async-start(bf16[2,32,2,32,1,128]{5,3,0,2,4,1:T(8,128)(2,1)} %bitcast.3), calls=%async_computation | async-start | bytes 2097152 | tf_op jit(solution)/shard_map/all_to_all | solution.py:105
  19.1 0.8 reshape.156
  19.9 0.8 reshape.161
  20.9 1.0 constant_dynamic-slice_fusion.6
  21.9 20.6 %all-to-all-done = bf16[2,32,2,32,1,128]{5,3,0,2,4,1:T(8,128)(2,1)S(1)} async-done(((bf16[2,32,2,32,1,128]{5,3,0,2,4,1:T(8,128)(2,1)}), bf16[2,32,2,32,1,128]{5,3,0,2,4,1:T(8,128)(2,1)S(1)}, u32[]{:S(2)}, u32[]{:S(2)}) %all-to-all-start) | async-done | bytes 1048608 | tf_op jit(solution)/shard_map/all_to_all | solution.py:105
  42.8 84.7 %while.26 = (s32[]{:T(128)}, f32[128,4,512]{2,0,1:T(8,128)S(1)}, s32[]{:T(128)}, s32[32]{0:T(128)S(1)}, s32[]{:T(128)}, /*index=5*/bf16[2,32,32,128]{3,1,0,2:T(8...) while((s32[]{:T(128)}, f32[128,4,512]{2,0,1:T(8,128)S(1)}, ...), condition=%wide.region_1.2_spmd.clone.clone, body=%wide.region_0.1_spmd.clone.clone.sunk | while | flops 37333684 | bytes 5670299 | solution.py:75
  46.5 0.7 fusion.309
  47.2 1.1 fusion.310
  50.0 1.1 fusion.311
  53.0 1.1 fusion.312
  55.9 1.1 fusion.313
  58.9 1.1 fusion.314
  62.0 1.1 fusion.315
  64.7 1.1 fusion.316
  67.9 1.1 fusion.317
  69.8 1.3 convolution_add_fusion.4
  74.7 0.7 fusion.309
  75.5 1.1 fusion.310
  78.3 1.1 fusion.311
  81.2 1.1 fusion.312
  84.2 1.1 fusion.313
  87.2 1.1 fusion.314
  90.2 1.1 fusion.315
  93.0 1.1 fusion.316
  96.2 1.1 fusion.317
  98.0 1.3 convolution_add_fusion.4
  103.0 0.7 fusion.309
  103.7 1.1 fusion.310
  106.5 1.1 fusion.311
  109.5 1.1 fusion.312
  112.4 1.1 fusion.313
  115.4 1.1 fusion.314
  118.4 1.1 fusion.315
  121.2 1.1 fusion.316
  124.4 1.1 fusion.317
  126.2 1.3 convolution_add_fusion.4
  128.3 56.6 %while.27 = (s32[]{:T(128)}, f32[128,4,512]{2,0,1:T(8,128)S(1)}, s32[]{:T(128)}, s32[32]{0:T(128)S(1)}, s32[]{:T(128)}, /*index=5*/bf16[2,32,32,128]{3,1,0,2:T(8...) while((s32[]{:T(128)}, f32[128,4,512]{2,0,1:T(8,128)S(1)}, ...), condition=%wide.region_3.4_spmd.clone.clone, body=%wide.region_2.3_spmd.clone.clone.sunk | while | flops 37333684 | bytes 5670299 | solution.py:75
  132.0 0.7 fusion.342
  132.8 1.1 fusion.343
  135.6 1.1 fusion.344
  138.5 1.1 fusion.345
  141.5 1.1 fusion.346
  144.5 1.1 fusion.347
  147.5 1.1 fusion.348
  150.3 1.1 fusion.349
  153.5 1.1 fusion.350
  155.4 1.3 convolution_add_fusion.5
  161.1 1.1 fusion.343
  163.9 1.1 fusion.344
  166.8 1.1 fusion.345
  169.8 1.1 fusion.346
  172.8 1.1 fusion.347
  175.8 1.1 fusion.348
  178.6 1.1 fusion.349
  181.8 1.1 fusion.350
  183.6 1.3 convolution_add_fusion.5
  185.6 1.9 pad_maximum_fusion.2
  189.0 87.8 %all-reduce.3.cloned.1.call-done = f32[128,2,4,512]{3,2,1,0:T(4,128)} async-done(((f32[128,2,4,512]{3,2,1,0:T(4,128)}), f32[128,2,4,512]{3,2,1,0:T(4,128)}) %all-reduce.3.cloned.1.call-update) | async-done | bytes 2097168
  276.8 1.0 fusion.214
  278.0 13.4 %all_gather.3 = bf16[16,8,4,128]{3,0,2,1:T(8,128)(2,1)S(1)} all-gather(bf16[16,2,4,128]{3,0,2,1:T(8,128)(2,1)S(1)} %copy.52), channel_id=1, replica_groups=mesh['facet'=4,'chan'=8] {'facet'}, dimensions={1}, use_global_device_ids=true | all-gather | bytes 163840 | tf_op jit(solution)/shard_map/all_gather | solution.py:131
  292.0 9.7 %scatter-add.6 = f32[16,2,4,512]{3,1,2,0:T(2,128)S(1)} dynamic-update-slice(f32[16,2,4,512]{3,1,2,0:T(2,128)S(1)} %copy.55, f32[16,2,4,64]{3,1,2,0:T(2,128)S(1)} %slice_add_fusion.1, s32[]{:T(128)} %constant.186.clone.1, s32[]{:T(128)} %constant.186.clone.1, s32[]{:T(128)} %constant.186.clone.1, s32[]{:T(128)} %constant.202.clone.1) | dynamic-update-slice | bytes 65540 | tf_op jit(solution)/shard_map/scatter-add | solution.py:142
  301.9 9.6 %scatter-add.9 = f32[16,2,4,512]{3,1,2,0:T(2,128)S(1)} dynamic-update-slice(f32[16,2,4,512]{3,1,2,0:T(2,128)S(1)} %scatter-add.6, f32[16,2,4,64]{3,1,2,0:T(2,128)S(1)} %slice_add_fusion, s32[]{:T(128)} %constant.186.clone.1, s32[]{:T(128)} %constant.186.clone.1, s32[]{:T(128)} %constant.186.clone.1, s32[]{:T(128)} %constant.203.clone.1) | dynamic-update-slice | bytes 65540 | tf_op jit(solution)/shard_map/scatter-add | solution.py:143
  311.5 0.8 copy.56
  (72 shorter events, 17.3 us)
Async XLA Ops:
  6.5 181.0 %copy-start = (s32[8,4]{0,1:T(4,128)S(1)}, s32[8,4]{0,1:T(4,128)}, u32[]{:S(2)}) copy-start(s32[8,4]{0,1:T(4,128)} %param.21) | copy-start | bytes 388
  9.0 33.5 %all-to-all-start = ((bf16[2,32,2,32,1,128]{5,3,0,2,4,1:T(8,128)(2,1)}), bf16[2,32,2,32,1,128]{5,3,0,2,4,1:T(8,128)(2,1)S(1)}, u32[]{:S(2)}, u32[]{:S(2)}) async-start(bf16[2,32,2,32,1,128]{5,3,0,2,4,1:T(8,128)(2,1)} %bitcast.3), calls=%async_computation | async-start | bytes 2097152 | tf_op jit(solution)/shard_map/all_to_all | solution.py:105
  16.4 260.4 %all-reduce.3.cloned.1.call-start = ((), (), s32[]{:S(2)}) async-start(), calls=%async_computation.1 | async-start | bytes 4194304
  184.9 2.8 copy-start.1
Sparse Core Ops, SparseCore 0:
  187.6 89.1 all-reduce.2
where the time goes:
time: 322 us; the launch traced here: 319 us
  waiting for transfers between devices  108 us (34%)
  loops' own time  75.9 us (24%)
  matrix products  57.8 us (18%)
  local copies, waits for them, and re-layouts  32.9 us (10%)
  between operations  15.6 us (5%)
  blocking collectives  13.4 us (4%)
  other arithmetic  7.59 us (2%)
  starting transfers between devices  7.37 us (2%)
    unnamed x2, waiting for transfers between devices  87.8 us
    another operation x2, loops' own time, grid_facet(): return lax.fori_loop(0, trip_count, accumulate, start_grid)  75.9 us
    dot_general x40, matrix products, project_rows(): jnp.dot(row_item, matrix, preferred_element_type=jnp.float32)  43.9 us
    all_to_all x1, waiting for transfers between devices, local(): lax.all_to_all(flattened, ('facet', 'chan'), split_axis=1, concat_axis=4,...  20.6 us
    all_gather x1, blocking collectives, local(): lax.all_gather(strips.astype(jnp.bfloat16), 'facet', axis=1, tiled=True)  13.4 us
    scatter-add x2, local copies, waits for them, and re-layouts, local(): joined.at[..., 2 * tile_cells - edge_cells:].add(blended[..., edge_cells:])  10.4 us
    scatter-add x1, local copies, waits for them, and re-layouts, local(): summed.at[..., tile_cells - edge_cells:tile_cells]  9.66 us
    all_to_all x1, starting transfers between devices, local(): lax.all_to_all(flattened, ('facet', 'chan'), split_axis=1, concat_axis=4,...  7.33 us
  transfers between devices with their start and end apart: 2, of which 2 were waited for; matrix products, arithmetic and copies ran while one was open for 2% of the time, Pallas kernels for 0%

commit v1 on v0

--- a/solution.py
+++ b/solution.py
@@ -102,7 +102,15 @@
     my_live = jnp.clip((counts - chan_index + n_chan - 1) // n_chan, 0, blk_dev)
     position = jnp.arange(channels, dtype=jnp.int32)
     flattened = arranged.reshape(halves, n_facet * n_chan, fac_dev, blk_dev, ch_dev, block_vis)
-    received = lax.all_to_all(flattened, ("facet", "chan"), split_axis=1, concat_axis=4, tiled=True)
+    received = jnp.concatenate(
+        lax.all_to_all(
+            jnp.stack(jnp.split(flattened, lax.axis_size(("facet", "chan")), axis=1)),
+            ("facet", "chan"),
+            0,
+            0,
+        ),
+        axis=4,
+    )
     local_vis = received.reshape(halves, fac_dev, blk_dev, channels, block_vis)
     freq_turn = 2.0 * math.pi * (1.0 + 0.5 * position.astype(jnp.float32) / channels)
     avg_matrix = (

time: 322 us -> 341 us (1.059)
  local copies, waits for them, and re-layouts: 32.9 us -> 51.3 us
    unnamed x5 -> x36, local copies, waits for them, and re-layouts: 0.59 us -> 19.3 us
  transfers between devices with their start and end apart: 2 -> 2, of which waited for: 2 -> 2; matrix products, arithmetic and copies ran while one was open for 2% -> 1% of each run, Pallas kernels for 0% -> 0%
where the time goes in v1:
time: 341 us; the launch traced here: 338 us
  waiting for transfers between devices  108 us (32%)
  loops' own time  75.9 us (22%)
  matrix products  57.8 us (17%)
  local copies, waits for them, and re-layouts  51.3 us (15%)
  between operations  15.7 us (5%)
  blocking collectives  13.4 us (4%)
  other arithmetic  7.59 us (2%)
  starting transfers between devices  7.37 us (2%)
    unnamed x2, waiting for transfers between devices  87.8 us
    another operation x2, loops' own time, grid_facet(): return lax.fori_loop(0, trip_count, accumulate, start_grid)  75.9 us
    dot_general x40, matrix products, project_rows(): jnp.dot(row_item, matrix, preferred_element_type=jnp.float32)  43.9 us
    all_to_all x1, waiting for transfers between devices, local(): lax.all_to_all(jnp.stack(jnp.split(flattened, lax.axis_size(('facet', 'ch...  20.6 us
    unnamed x36, local copies, waits for them, and re-layouts  19.3 us
    all_gather x1, blocking collectives, local(): lax.all_gather(strips.astype(jnp.bfloat16), 'facet', axis=1, tiled=True)  13.4 us
    scatter-add x2, local copies, waits for them, and re-layouts, local(): joined.at[..., 2 * tile_cells - edge_cells:].add(blended[..., edge_cells:])  10.4 us
    scatter-add x1, local copies, waits for them, and re-layouts, local(): summed.at[..., tile_cells - edge_cells:tile_cells]  9.66 us
  transfers between devices with their start and end apart: 2, of which 2 were waited for; matrix products, arithmetic and copies ran while one was open for 1% of the time, Pallas kernels for 0%

profile of v1, /device:TPU:0, one launch (start us, length us, event | category | flops | bytes accessed | tf_op | source)
XLA Modules:
  0.0 337.6 jit_solution(15578383240599463969)
XLA Ops:
  6.5 1.5 copy.81
  27.4 7.3 %all-to-all-start = ((bf16[32,2,1,2,32,1,128]{6,4,3,1,5,2,0:T(8,128)(2,1)}), bf16[32,2,1,2,32,1,128]{6,4,3,1,5,2,0:T(8,128)(2,1)S(1)}, u32[]{:S(2)}, u32[]{:S(2)}) async-start(bf16[32,2,1,2,32,1,128]{6,4,3,1,5,2,0:T(8,128)(2,1)} %constant_dynamic-update-slice_fusion), calls=%async_computation | async-start | bytes 2097152 | tf_op jit(solution)/shard_map/all_to_all | solution.py:106
  37.5 0.8 reshape.155
  38.3 0.8 reshape.160
  39.3 1.0 constant_dynamic-slice_fusion.6
  40.3 20.6 %all-to-all-done = bf16[32,2,1,2,32,1,128]{6,4,3,1,5,2,0:T(8,128)(2,1)S(1)} async-done(((bf16[32,2,1,2,32,1,128]{6,4,3,1,5,2,0:T(8,128)(2,1)}), bf16[32,2,1,2,32,1,128]{6,4,3,1,5,2,0:T(8,128)(2,1)S(1)}, u32[]{:S(2)}, u32[]{:S(2)}) %all-to-all-start) | async-done | bytes 1048608 | tf_op jit(solution)/shard_map/all_to_all | solution.py:106
  61.2 84.7 %while.26 = (s32[]{:T(128)}, f32[128,4,512]{2,0,1:T(8,128)S(1)}, s32[]{:T(128)}, s32[32]{0:T(128)S(1)}, s32[]{:T(128)}, /*index=5*/bf16[2,32,32,128]{3,1,0,2:T(8...) while((s32[]{:T(128)}, f32[128,4,512]{2,0,1:T(8,128)S(1)}, ...), condition=%wide.region_1.2_spmd.clone.clone, body=%wide.region_0.1_spmd.clone.clone.sunk | while | flops 37333684 | bytes 5670299 | solution.py:75
  64.9 0.7 fusion.309
  65.7 1.1 fusion.310
  68.5 1.1 fusion.311
  71.4 1.1 fusion.312
  74.4 1.1 fusion.313
  77.4 1.1 fusion.314
  80.4 1.1 fusion.315
  83.2 1.1 fusion.316
  86.4 1.1 fusion.317
  88.2 1.3 convolution_add_fusion.4
  93.2 0.7 fusion.309
  93.9 1.1 fusion.310
  96.7 1.1 fusion.311
  99.7 1.1 fusion.312
  102.6 1.1 fusion.313
  105.6 1.1 fusion.314
  108.6 1.1 fusion.315
  111.4 1.1 fusion.316
  114.6 1.1 fusion.317
  116.4 1.3 convolution_add_fusion.4
  121.4 0.7 fusion.309
  122.2 1.1 fusion.310
  125.0 1.1 fusion.311
  127.9 1.1 fusion.312
  130.9 1.1 fusion.313
  133.9 1.1 fusion.314
  136.9 1.1 fusion.315
  139.7 1.1 fusion.316
  142.9 1.1 fusion.317
  144.7 1.3 convolution_add_fusion.4
  146.8 56.6 %while.27 = (s32[]{:T(128)}, f32[128,4,512]{2,0,1:T(8,128)S(1)}, s32[]{:T(128)}, s32[32]{0:T(128)S(1)}, s32[]{:T(128)}, /*index=5*/bf16[2,32,32,128]{3,1,0,2:T(8...) while((s32[]{:T(128)}, f32[128,4,512]{2,0,1:T(8,128)S(1)}, ...), condition=%wide.region_3.4_spmd.clone.clone, body=%wide.region_2.3_spmd.clone.clone.sunk | while | flops 37333684 | bytes 5670299 | solution.py:75
  151.2 1.1 fusion.343
  154.0 1.1 fusion.344
  157.0 1.1 fusion.345
  159.9 1.1 fusion.346
  162.9 1.1 fusion.347
  165.9 1.1 fusion.348
  168.7 1.1 fusion.349
  171.9 1.1 fusion.350
  173.8 1.3 convolution_add_fusion.5
  178.8 0.7 fusion.342
  179.5 1.1 fusion.343
  182.3 1.1 fusion.344
  185.3 1.1 fusion.345
  188.2 1.1 fusion.346
  191.2 1.1 fusion.347
  194.3 1.1 fusion.348
  197.0 1.1 fusion.349
  200.2 1.1 fusion.350
  202.1 1.3 convolution_add_fusion.5
  204.1 1.9 pad_maximum_fusion.2
  207.5 87.8 %all-reduce.3.cloned.1.call-done = f32[128,2,4,512]{3,2,1,0:T(4,128)} async-done(((f32[128,2,4,512]{3,2,1,0:T(4,128)}), f32[128,2,4,512]{3,2,1,0:T(4,128)}) %all-reduce.3.cloned.1.call-update) | async-done | bytes 2097168
  295.3 1.0 fusion.214
  296.5 13.4 %all_gather.3 = bf16[16,8,4,128]{3,0,2,1:T(8,128)(2,1)S(1)} all-gather(bf16[16,2,4,128]{3,0,2,1:T(8,128)(2,1)S(1)} %copy.87), channel_id=1, replica_groups=mesh['facet'=4,'chan'=8] {'facet'}, dimensions={1}, use_global_device_ids=true | all-gather | bytes 163840 | tf_op jit(solution)/shard_map/all_gather | solution.py:139
  310.5 9.7 %scatter-add.6 = f32[16,2,4,512]{3,1,2,0:T(2,128)S(1)} dynamic-update-slice(f32[16,2,4,512]{3,1,2,0:T(2,128)S(1)} %copy.90, f32[16,2,4,64]{3,1,2,0:T(2,128)S(1)} %slice_add_fusion.1, s32[]{:T(128)} %constant.186.clone.1, s32[]{:T(128)} %constant.186.clone.1, s32[]{:T(128)} %constant.186.clone.1, s32[]{:T(128)} %constant.202.clone.1) | dynamic-update-slice | bytes 65540 | tf_op jit(solution)/shard_map/scatter-add | solution.py:150
  320.4 9.6 %scatter-add.9 = f32[16,2,4,512]{3,1,2,0:T(2,128)S(1)} dynamic-update-slice(f32[16,2,4,512]{3,1,2,0:T(2,128)S(1)} %scatter-add.6, f32[16,2,4,64]{3,1,2,0:T(2,128)S(1)} %slice_add_fusion, s32[]{:T(128)} %constant.186.clone.1, s32[]{:T(128)} %constant.186.clone.1, s32[]{:T(128)} %constant.186.clone.1, s32[]{:T(128)} %constant.203.clone.1) | dynamic-update-slice | bytes 65540 | tf_op jit(solution)/shard_map/scatter-add | solution.py:151
  329.9 0.8 copy.91
  (104 shorter events, 36.7 us)
Async XLA Ops:
  6.5 199.5 %copy-start = (s32[8,4]{0,1:T(4,128)S(1)}, s32[8,4]{0,1:T(4,128)}, u32[]{:S(2)}) copy-start(s32[8,4]{0,1:T(4,128)} %param.21) | copy-start | bytes 388
  27.4 33.5 %all-to-all-start = ((bf16[32,2,1,2,32,1,128]{6,4,3,1,5,2,0:T(8,128)(2,1)}), bf16[32,2,1,2,32,1,128]{6,4,3,1,5,2,0:T(8,128)(2,1)S(1)}, u32[]{:S(2)}, u32[]{:S(2)}) async-start(bf16[32,2,1,2,32,1,128]{6,4,3,1,5,2,0:T(8,128)(2,1)} %constant_dynamic-update-slice_fusion), calls=%async_computation | async-start | bytes 2097152 | tf_op jit(solution)/shard_map/all_to_all | solution.py:106
  34.7 260.5 %all-reduce.3.cloned.1.call-start = ((), (), s32[]{:S(2)}) async-start(), calls=%async_computation.1 | async-start | bytes 4194304
  203.4 2.8 copy-start.1
Sparse Core Ops, SparseCore 0:
  206.1 89.1 all-reduce.2
